TPU v7x, 32 devices: a whole 2x2x4 slice. The times are simulated.
32 devices in a mesh: row: 4 (over z), col: 8 (over y, x, core).
Axes of the slice: x: 2, y: 2, z: 4, core: 2. Of those that a mesh axis runs over, the one named last changes fastest.
Arguments:
- neighbor: int32 [32, 3072, 3072], P(None, 'col', 'row'), may hold values from 0 to 1, as said below
- true_coords: float32 [32, 3, 3072], P(None, None, ('row', 'col')), as said below
- pred_coords: float32 [32, 3, 3072], P(None, None, ('row', 'col')), as said below
- residue_mask: int32 [32, 3072], P(None, ('row', 'col')), may hold values from 0 to 1, as said below
- single: bfloat16 [32, 3072, 384], P(None, ('row', 'col'))
- ln_gain: float32 [384], replicated, may hold values from 0.1 to 1.9
- w_hidden: bfloat16 [384, 128], replicated, may hold values from -0.3125 to 0.3125
- b_hidden: float32 [128], replicated, may hold values from -3 to 3
- w_mid: bfloat16 [128, 128], replicated, may hold values from -0.5 to 0.5
- b_mid: float32 [128], replicated, may hold values from -3 to 3
- w_logits: bfloat16 [128, 50], replicated, may hold values from -1.5 to 1.5
- b_logits: float32 [50], replicated, may hold values from -4 to 4
Outputs:
- lddt_score: float32 [32, 3072], P(None, ('row', 'col'))
- residue_loss: float32 [32, 3072], P(None, ('row', 'col'))
- total_loss: float32 [], replicated
Inputs may be any that keep to these rules, and one draw needn't show every extreme that they name: `neighbor`: 0 or 1; 0 where j == i; 1 wherever 0 < |i - j| <= 8. `residue_mask`: per structure, 1 on a leading run of 1536 or more residues and 0 after it. `true_coords`: positions in angstroms. `pred_coords`: positions in angstroms.
All inputs are finite; a program needn't handle non-finite values.
Results may differ from a plain program's by a relative error of at most 0.00098.
Values sent between devices are 32-bit elements; how exact they have to be, the bound alone decides.
A program may use at most 128 MiB of HBM per device.

v0:
```python
import jax
import jax.numpy as jnp
from jax import lax
from jax.sharding import PartitionSpec as P

L = 3072
THRESHOLDS = (0.5, 1.0, 2.0, 4.0)


def from_root(shard, axis, root):
    mine = lax.axis_index(axis) == root
    return lax.psum(jnp.where(mine, shard, jnp.zeros_like(shard)), axis)


def tile_dist(rows_block, cols_block):
    total = (cols_block[:, 0, :, None] - rows_block[:, 0, None, :]) ** 2
    total = total + (cols_block[:, 1, :, None] - rows_block[:, 1, None, :]) ** 2
    total = total + (cols_block[:, 2, :, None] - rows_block[:, 2, None, :]) ** 2
    return jnp.sqrt(total + 1e-10)


def head_loss(lddt_value, single, ln_gain, w_hidden, b_hidden, w_mid, b_mid, w_logits, b_logits):
    features = single.astype(jnp.float32)
    average = jnp.mean(features, axis=-1, keepdims=True)
    centred = features - average
    variance = jnp.mean(centred * centred, axis=-1, keepdims=True)
    normed = (centred * lax.rsqrt(variance + 1e-05) * ln_gain).astype(jnp.bfloat16)
    first_hidden = jax.nn.relu(
        jnp.dot(normed, w_hidden, preferred_element_type=jnp.float32) + b_hidden
    ).astype(jnp.bfloat16)
    second_hidden = jax.nn.relu(
        jnp.dot(first_hidden, w_mid, preferred_element_type=jnp.float32) + b_mid
    ).astype(jnp.bfloat16)
    logits = jnp.dot(second_hidden, w_logits, preferred_element_type=jnp.float32) + b_logits
    log_total = jnp.log(jnp.sum(jnp.exp(logits), axis=-1))
    bins = logits.shape[-1]
    centers = (jnp.arange(bins).astype(jnp.float32) + 0.5) / bins
    closeness = jnp.exp(-((lddt_value[..., None] - centers) ** 2) * (bins * bins * 0.5))
    target = closeness / jnp.sum(closeness, axis=-1, keepdims=True)
    return log_total - jnp.sum(target * logits, axis=-1)


def local(
    neighbor,
    true_coords,
    pred_coords,
    residue_mask,
    single,
    ln_gain,
    w_hidden,
    b_hidden,
    w_mid,
    b_mid,
    w_logits,
    b_logits,
):
    valid = residue_mask.astype(jnp.float32)
    own_len = residue_mask.shape[1]
    stacked = jnp.concatenate([true_coords, pred_coords, valid[:, None, :]], axis=1)
    row_count = lax.axis_size("row")
    col_count = lax.axis_size("col")
    rows_len = L // row_count
    cols_len = L // col_count
    col_index = lax.axis_index("col")
    rows_part = lax.all_gather(stacked, "col", axis=2, tiled=True)
    offset = col_index * cols_len % rows_len
    column_piece = lax.dynamic_slice_in_dim(rows_part, offset, cols_len, 2)
    source_row = col_index * cols_len // rows_len
    cols_part = from_root(column_piece, "row", source_row)
    true_dist = tile_dist(rows_part[:, 0:3], cols_part[:, 0:3])
    pred_dist = tile_dist(rows_part[:, 3:6], cols_part[:, 3:6])
    mismatch = jnp.abs(pred_dist - true_dist)
    scores = jnp.zeros_like(mismatch)
    for threshold in THRESHOLDS:
        scores = scores + jax.nn.sigmoid(4.0 * (threshold - mismatch))
    scores = 0.25 * scores
    weights = neighbor.astype(jnp.float32) * rows_part[:, 6, None, :] * cols_part[:, 6, :, None]
    preserved = jnp.sum(weights * scores, axis=1)
    neighbors = jnp.sum(weights, axis=1)
    preserved_all, neighbors_all = lax.psum((preserved, neighbors), "col")
    preserved_own = lax.dynamic_slice_in_dim(preserved_all, col_index * own_len, own_len, 1)
    neighbors_own = lax.dynamic_slice_in_dim(neighbors_all, col_index * own_len, own_len, 1)
    lddt_score = preserved_own / jnp.maximum(neighbors_own, 1.0)
    residue_loss = valid * head_loss(
        lddt_score, single, ln_gain, w_hidden, b_hidden, w_mid, b_mid, w_logits, b_logits
    )
    loss_sum, valid_sum = lax.psum((jnp.sum(residue_loss), jnp.sum(valid)), ("row", "col"))
    total_loss = loss_sum / valid_sum
    return (lddt_score, residue_loss, total_loss)


def solution(mesh):
    placed = (
        P(None, "col", "row"),
        P(None, None, ("row", "col")),
        P(None, None, ("row", "col")),
        P(None, ("row", "col")),
        P(None, ("row", "col"), None),
        P(),
        P(),
        P(),
        P(),
        P(),
        P(),
        P(),
    )
    return jax.shard_map(
        local,
        mesh=mesh,
        in_specs=placed,
        out_specs=(P(None, ("row", "col")), P(None, ("row", "col")), P()),
        check_vma=False,
    )
```

profile of v0, /device:TPU:0, one launch (start us, length us, event | category | flops | bytes accessed | tf_op | source)
XLA Modules:
  0.0 312.7 jit_solution(15335422747212448188)
XLA Ops:
  7.3 0.7 convert_bitcast_fusion
  8.0 0.8 pad_maximum_fusion
  8.8 0.9 copy.33
  9.7 21.3 %all_gather.3 = f32[32,7,768]{0,1,2:T(8,128)S(1)} all-gather(f32[32,7,96]{0,1,2:T(8,128)} %copy.33), channel_id=1, replica_groups=mesh['row'=4,'col'=8] {'col'}, dimensions={2}, use_global_device_ids=true | all-gather | bytes 774144 | tf_op jit(solution)/shard_map/all_gather | solution.py:65
  31.0 1.3 dynamic-slice_select_fusion
  32.4 3.3 %fusion.31 = (f32[32,1,768]{0,1,2:T(1,128)}, f32[32,1,768]{0,1,2:T(1,128)}, f32[32,1,768]{0,1,2:T(1,128)}, f32[32,1,768]{0,1,2:T(1,128)}, f32[32,1,768]{0,1,2:T(...) fusion(f32[32,7,768]{0,1,2:T(8,128)S(1)} %all_gather.3), kind=kLoop, calls=%fused_computation.43 | loop fusion | bytes 1376256 | tf_op jit(solution)/shard_map/slice | solution.py:77
  35.6 2.3 convert_reduce_fusion
  37.9 2.8 fusion.4
  40.8 3.2 %maximum_convert_fusion = bf16[32,96,128]{2,1,0:T(8,128)(2,1)S(1)} fusion(bf16[32,96,384]{2,1,0:T(8,128)(2,1)} %param.16, f32[384]{0:T(512)} %param.17, f32[32,96]{1,0:T(8,128)S(1)} %add_rsqrt_fusion, f32[32,96]{1,0:T(8,128)S(1)} %broadcast_multiply_fusion, f32[128]{0:T(128)} %param.21, f32[128]{0:T(128)} %param.19, bf16[384,128]{1,0:T(8,128)(2,1)S(1)} %copy-done, ...), kind=kOutput, calls=%fused_computation.15 | convolution fusion | flops 410910720 | bytes 3303936 | tf_op jit(solution)/shard_map/dot_general | solution.py:32
  44.0 1.1 copy.34
  45.1 1.1 copy.37
  46.2 1.1 copy.39
  47.4 1.1 copy.41
  48.5 1.1 copy.43
  49.7 1.1 copy.45
  50.8 1.1 copy.47
  51.9 1.4 exponential_reduce_fusion
  53.4 48.4 %all-reduce.5.cloned.1.call-done = f32[32,7,384]{0,1,2:T(8,128)} async-done(((f32[32,7,384]{0,1,2:T(8,128)}), f32[32,7,384]{0,1,2:T(8,128)}) %all-reduce.5.cloned.1.call-update) | async-done | bytes 344080 | tf_op jit(solution)/shard_map/psum | solution.py:12
  101.7 6.8 %fusion.32 = (f32[32,1,384]{0,1,2:T(1,128)S(1)}, f32[32,1,384]{0,1,2:T(1,128)S(1)}, f32[32,1,384]{0,1,2:T(1,128)S(1)}, f32[32,1,384]{0,1,2:T(1,128)S(1)}, f32[32...) fusion(f32[32,7,384]{0,1,2:T(8,128)} %all-reduce.5.cloned.1.call-done), kind=kLoop, calls=%fused_computation.44 | loop fusion | bytes 688128 | tf_op jit(solution)/shard_map/slice | solution.py:77
  108.5 0.1 copy.35
  108.6 0.1 copy.36
  108.7 0.1 copy.38
  108.8 0.1 copy.40
  108.9 0.1 copy.42
  109.1 0.1 copy.44
  109.2 0.1 copy.46
  109.3 98.8 %multiply_reduce_fusion = (f32[32,768]{1,0:T(8,128)}, f32[32,768]{1,0:T(8,128)}) fusion(s32[32,384,768]{2,1,0:T(8,128)} %param.12, f32[32,768]{1,0:T(8,128)S(1)} %copy.47, f32[32,384]{1,0:T(8,128)S(1)} %copy.46, f32[32,768]{1,0:T(8,128)S(1)} %copy.45, f32[32,384]{1,0:T(8,128)S(1)} %copy.44, f32[32,768]{1,0:T(8,128)S(1)} %copy.43, f32[32,384]{1,0:T(8,128)S(1)} %copy.42, ...), kind=kLoop, calls=%fused_computation.1 | loop fusion | flops 471810048 | bytes 38977536 | tf_op jit(solution)/shard_map/reduce_sum | solution.py:78
  208.2 53.1 %all-reduce.7.cloned.1.call-done = (f32[32,768]{1,0:T(8,128)}, f32[32,768]{1,0:T(8,128)}) async-done(((f32[32,768]{1,0:T(8,128)}, f32[32,768]{1,0:T(8,128)}), (f32[32,768]{1,0:T(8,128)}, f32[32,768]{1,0:T(8,128)})) %all-reduce.7.cloned.1.call-update) | async-done | bytes 196624 | tf_op jit(solution)/shard_map/psum | solution.py:80
  261.3 0.9 maximum_divide_fusion
  262.1 0.4 fusion.33
  262.6 1.3 fusion.30
  263.9 39.6 %all-reduce = (f32[]{:T(128)}, f32[]{:T(128)}) all-reduce(f32[]{:T(128)} %get-tuple-element.12, f32[]{:T(128)} %get-tuple-element.28), channel_id=1, replica_groups=mesh['row'=4,'col'=8] {'row','col'}, use_global_device_ids=true, to_apply=%region_11.12 | all-reduce | flops 2 | bytes 16 | tf_op jit(solution)/shard_map/psum | solution.py:87
  (13 shorter events, 0.2 us)
Async XLA Ops:
  7.2 33.6 %copy-start = (bf16[384,128]{1,0:T(8,128)(2,1)S(1)}, bf16[384,128]{1,0:T(8,128)(2,1)}, u32[]{:S(2)}) copy-start(bf16[384,128]{1,0:T(8,128)(2,1)} %param.18) | copy-start | bytes 294916
  7.2 94.6 %all-reduce.5.cloned.1.call-start = ((), (), s32[]{:S(2)}) async-start(), calls=%async_computation | async-start | bytes 3145728 | tf_op jit(solution)/shard_map/psum | solution.py:12
  32.3 228.9 %all-reduce.7.cloned.1.call-start = ((), (), s32[]{:S(2)}) async-start(), calls=%async_computation.1 | async-start | bytes 393216 | tf_op jit(solution)/shard_map/psum | solution.py:80
  109.3 153.3 %copy-start.1 = (s32[32,96]{1,0:T(8,128)S(1)}, s32[32,96]{1,0:T(8,128)}, u32[]{:S(2)}) copy-start(s32[32,96]{1,0:T(8,128)} %param.15) | copy-start | bytes 36868
  262.1 42.6 %copy-start.2 = (f32[32,96]{1,0:T(8,128)}, f32[32,96]{1,0:T(8,128)S(1)}, u32[]{:S(2)}) copy-start(f32[32,96]{1,0:T(8,128)S(1)} %maximum_divide_fusion) | copy-start | bytes 36868
Sparse Core Ops, SparseCore 0:
  32.5 69.2 all-reduce.4
  208.3 52.9 all-reduce.6
where the time goes:
time: 314 us; the launch traced here: 313 us
  other arithmetic  109 us (35%)
  waiting for transfers between devices  102 us (32%)
  blocking collectives  60.8 us (19%)
  local copies, waits for them, and re-layouts  19.7 us (6%)
  between operations  16.6 us (5%)
  matrix products  4.59 us (1%)
    reduce_sum x1, other arithmetic, local(): preserved = jnp.sum(weights * scores, axis=1)  98.8 us
    psum x1, waiting for transfers between devices, local(): preserved_all, neighbors_all = lax.psum((preserved, neighbors), 'col')  53.1 us
    psum x1, waiting for transfers between devices, from_root(): return lax.psum(jnp.where(mine, shard, jnp.zeros_like(shard)), axis)  48.4 us
    psum x1, blocking collectives, local(): lax.psum((jnp.sum(residue_loss), jnp.sum(valid)), ('row', 'col'))  39.6 us
    all_gather x1, blocking collectives, local(): rows_part = lax.all_gather(stacked, 'col', axis=2, tiled=True)  21.3 us
    slice x1, local copies, waits for them, and re-layouts, local(): cols_part[:, 6, :, None]  6.78 us
  transfers between devices with their start and end apart: 2, of which 2 were waited for; matrix products, arithmetic and copies ran while one was open for 7% of the time, Pallas kernels for 0%

commit v1 on v0

--- a/solution.py
+++ b/solution.py
@@ -5,6 +5,7 @@
 
 L = 3072
 THRESHOLDS = (0.5, 1.0, 2.0, 4.0)
+define_stacks_all_over_axis = lambda tile_in: jax.lax.psum(jax.lax.psum(tile_in, "col"), "row")
 
 
 def from_root(shard, axis, root):
@@ -84,7 +85,7 @@
     residue_loss = valid * head_loss(
         lddt_score, single, ln_gain, w_hidden, b_hidden, w_mid, b_mid, w_logits, b_logits
     )
-    loss_sum, valid_sum = lax.psum((jnp.sum(residue_loss), jnp.sum(valid)), ("row", "col"))
+    loss_sum, valid_sum = define_stacks_all_over_axis((jnp.sum(residue_loss), jnp.sum(valid)))
     total_loss = loss_sum / valid_sum
     return (lddt_score, residue_loss, total_loss)
 

time: 314 us -> 299 us (0.952)
  blocking collectives: 60.8 us -> 46.1 us
    psum x1 -> x2, blocking collectives: 39.6 us -> 24.8 us  [the longest x1 12.5 us: jax.lax.psum(tile_in, 'col')]
where the time goes in v1:
time: 299 us; the launch traced here: 298 us
  other arithmetic  109 us (36%)
  waiting for transfers between devices  102 us (34%)
  blocking collectives  46.1 us (15%)
  local copies, waits for them, and re-layouts  19.7 us (7%)
  between operations  16.6 us (6%)
  matrix products  4.59 us (2%)
    reduce_sum x1, other arithmetic, local(): preserved = jnp.sum(weights * scores, axis=1)  98.8 us
    psum x1, waiting for transfers between devices, local(): preserved_all, neighbors_all = lax.psum((preserved, neighbors), 'col')  53.1 us
    psum x1, waiting for transfers between devices, from_root(): return lax.psum(jnp.where(mine, shard, jnp.zeros_like(shard)), axis)  48.4 us
    all_gather x1, blocking collectives, local(): rows_part = lax.all_gather(stacked, 'col', axis=2, tiled=True)  21.3 us
    psum x1, blocking collectives, jax.lax.psum(tile_in, 'col')  12.5 us
    psum x1, blocking collectives, jax.lax.psum(jax.lax.psum(tile_in, 'col'), 'row')  12.3 us
    slice x1, local copies, waits for them, and re-layouts, local(): cols_part[:, 6, :, None]  6.78 us
  transfers between devices with their start and end apart: 2, of which 2 were waited for; matrix products, arithmetic and copies ran while one was open for 7% of the time, Pallas kernels for 0%

profile of v1, /device:TPU:0, one launch (start us, length us, event | category | flops | bytes accessed | tf_op | source)
XLA Modules:
  0.0 297.8 jit_solution(2416281162743364807)
XLA Ops:
  7.3 0.7 convert_bitcast_fusion
  8.0 0.8 pad_maximum_fusion
  8.8 0.9 copy.33
  9.7 21.3 %all_gather.3 = f32[32,7,768]{0,1,2:T(8,128)S(1)} all-gather(f32[32,7,96]{0,1,2:T(8,128)} %copy.33), channel_id=1, replica_groups=mesh['row'=4,'col'=8] {'col'}, dimensions={2}, use_global_device_ids=true | all-gather | bytes 774144 | tf_op jit(solution)/shard_map/all_gather | solution.py:66
  31.0 1.3 dynamic-slice_select_fusion
  32.4 3.3 %fusion.31 = (f32[32,1,768]{0,1,2:T(1,128)}, f32[32,1,768]{0,1,2:T(1,128)}, f32[32,1,768]{0,1,2:T(1,128)}, f32[32,1,768]{0,1,2:T(1,128)}, f32[32,1,768]{0,1,2:T(...) fusion(f32[32,7,768]{0,1,2:T(8,128)S(1)} %all_gather.3), kind=kLoop, calls=%fused_computation.43 | loop fusion | bytes 1376256 | tf_op jit(solution)/shard_map/slice | solution.py:78
  35.6 2.3 convert_reduce_fusion
  37.9 2.8 fusion.4
  40.8 3.2 %maximum_convert_fusion = bf16[32,96,128]{2,1,0:T(8,128)(2,1)S(1)} fusion(bf16[32,96,384]{2,1,0:T(8,128)(2,1)} %param.16, f32[384]{0:T(512)} %param.17, f32[32,96]{1,0:T(8,128)S(1)} %add_rsqrt_fusion, f32[32,96]{1,0:T(8,128)S(1)} %broadcast_multiply_fusion, f32[128]{0:T(128)} %param.21, f32[128]{0:T(128)} %param.19, bf16[384,128]{1,0:T(8,128)(2,1)S(1)} %copy-done, ...), kind=kOutput, calls=%fused_computation.15 | convolution fusion | flops 410910720 | bytes 3303936 | tf_op jit(solution)/shard_map/dot_general | solution.py:33
  44.0 1.1 copy.34
  45.1 1.1 copy.37
  46.2 1.1 copy.39
  47.4 1.1 copy.41
  48.5 1.1 copy.43
  49.7 1.1 copy.45
  50.8 1.1 copy.47
  51.9 1.4 exponential_reduce_fusion
  53.4 48.4 %all-reduce.6.cloned.1.call-done = f32[32,7,384]{0,1,2:T(8,128)} async-done(((f32[32,7,384]{0,1,2:T(8,128)}), f32[32,7,384]{0,1,2:T(8,128)}) %all-reduce.6.cloned.1.call-update) | async-done | bytes 344080 | tf_op jit(solution)/shard_map/psum | solution.py:13
  101.7 6.8 %fusion.32 = (f32[32,1,384]{0,1,2:T(1,128)S(1)}, f32[32,1,384]{0,1,2:T(1,128)S(1)}, f32[32,1,384]{0,1,2:T(1,128)S(1)}, f32[32,1,384]{0,1,2:T(1,128)S(1)}, f32[32...) fusion(f32[32,7,384]{0,1,2:T(8,128)} %all-reduce.6.cloned.1.call-done), kind=kLoop, calls=%fused_computation.44 | loop fusion | bytes 688128 | tf_op jit(solution)/shard_map/slice | solution.py:78
  108.6 0.1 copy.36
  108.7 0.1 copy.38
  108.8 0.1 copy.40
  108.9 0.1 copy.42
  109.1 0.1 copy.44
  109.2 0.1 copy.46
  109.3 98.8 %multiply_reduce_fusion = (f32[32,768]{1,0:T(8,128)}, f32[32,768]{1,0:T(8,128)}) fusion(s32[32,384,768]{2,1,0:T(8,128)} %param.12, f32[32,768]{1,0:T(8,128)S(1)} %copy.47, f32[32,384]{1,0:T(8,128)S(1)} %copy.46, f32[32,768]{1,0:T(8,128)S(1)} %copy.45, f32[32,384]{1,0:T(8,128)S(1)} %copy.44, f32[32,768]{1,0:T(8,128)S(1)} %copy.43, f32[32,384]{1,0:T(8,128)S(1)} %copy.42, ...), kind=kLoop, calls=%fused_computation.1 | loop fusion | flops 471810048 | bytes 38977536 | tf_op jit(solution)/shard_map/reduce_sum | solution.py:79
  208.2 53.1 %all-reduce.8.cloned.1.call-done = (f32[32,768]{1,0:T(8,128)}, f32[32,768]{1,0:T(8,128)}) async-done(((f32[32,768]{1,0:T(8,128)}, f32[32,768]{1,0:T(8,128)}), (f32[32,768]{1,0:T(8,128)}, f32[32,768]{1,0:T(8,128)})) %all-reduce.8.cloned.1.call-update) | async-done | bytes 196624 | tf_op jit(solution)/shard_map/psum | solution.py:81
  261.3 0.9 maximum_divide_fusion
  262.1 0.4 fusion.33
  262.6 1.2 fusion.30
  263.8 12.5 %all-reduce = (f32[]{:T(128)}, f32[]{:T(128)}) all-reduce(f32[]{:T(128)} %get-tuple-element.14, f32[]{:T(128)} %get-tuple-element.30), channel_id=1, replica_groups=mesh['row'=4,'col'=8] {'col'}, use_global_device_ids=true, to_apply=%region_11.12 | all-reduce | flops 2 | bytes 16 | tf_op jit(solution)/shard_map/psum | solution.py:8
  276.3 12.3 %all-reduce.2 = (f32[]{:T(128)}, f32[]{:T(128)}) all-reduce(f32[]{:T(128)} %get-tuple-element.8, f32[]{:T(128)} %get-tuple-element.9), channel_id=1, replica_groups=mesh['row'=4,'col'=8] {'row'}, use_global_device_ids=true, to_apply=%region_12.13 | all-reduce | flops 2 | bytes 16 | tf_op jit(solution)/shard_map/psum | solution.py:8
  (14 shorter events, 0.2 us)
Async XLA Ops:
  7.2 33.6 %copy-start = (bf16[384,128]{1,0:T(8,128)(2,1)S(1)}, bf16[384,128]{1,0:T(8,128)(2,1)}, u32[]{:S(2)}) copy-start(bf16[384,128]{1,0:T(8,128)(2,1)} %param.18) | copy-start | bytes 294916
  7.2 94.6 %all-reduce.6.cloned.1.call-start = ((), (), s32[]{:S(2)}) async-start(), calls=%async_computation | async-start | bytes 3145728 | tf_op jit(solution)/shard_map/psum | solution.py:13
  32.3 228.9 %all-reduce.8.cloned.1.call-start = ((), (), s32[]{:S(2)}) async-start(), calls=%async_computation.1 | async-start | bytes 393216 | tf_op jit(solution)/shard_map/psum | solution.py:81
  109.3 153.3 %copy-start.1 = (s32[32,96]{1,0:T(8,128)S(1)}, s32[32,96]{1,0:T(8,128)}, u32[]{:S(2)}) copy-start(s32[32,96]{1,0:T(8,128)} %param.15) | copy-start | bytes 36868
  262.1 27.7 %copy-start.2 = (f32[32,96]{1,0:T(8,128)}, f32[32,96]{1,0:T(8,128)S(1)}, u32[]{:S(2)}) copy-start(f32[32,96]{1,0:T(8,128)S(1)} %maximum_divide_fusion) | copy-start | bytes 36868
Sparse Core Ops, SparseCore 0:
  32.5 69.2 all-reduce.5
  208.3 52.9 all-reduce.7
